TPU v7x, 8 devices: a whole 2x2x1 slice. The times are simulated.
8 devices in a mesh: dp: 1 (over z), ei: 2 (over y), eo: 4 (over x, core).
Axes of the slice: x: 2, y: 2, z: 1, core: 2. Of those that a mesh axis runs over, the one named last changes fastest.
Arguments:
- x_tokens: bfloat16 [16384, 1536], P(('dp', 'ei', 'eo'))
- expert_ids: int32 [16384, 6], P(('dp', 'ei', 'eo'))
- gate_vals: float32 [16384, 6], P(('dp', 'ei', 'eo'))
- w_gate: bfloat16 [64, 1536, 512], P(('ei', 'eo'))
- w_up: bfloat16 [64, 1536, 512], P(('ei', 'eo'))
- w_down: bfloat16 [64, 512, 1536], P(('ei', 'eo'))
- ws_gate: bfloat16 [1536, 1024], replicated
- ws_up: bfloat16 [1536, 1024], replicated
- ws_down: bfloat16 [1024, 1536], replicated
- dy_tokens: bfloat16 [16384, 1536], P(('dp', 'ei', 'eo'))
Outputs:
- output 1: bfloat16 [16384, 1536], P(('dp', 'ei', 'eo'))
- output 2: bfloat16 [16384, 1536], P(('dp', 'ei', 'eo'))
- output 3: float32 [16384, 6], P(('dp', 'ei', 'eo'))
- output 4: bfloat16 [64, 1536, 512], P(('dp', 'ei', 'eo'))
- output 5: bfloat16 [64, 1536, 512], P(('dp', 'ei', 'eo'))
- output 6: bfloat16 [64, 512, 1536], P(('dp', 'ei', 'eo'))
- output 7: float32 [1536, 1024], P('dp')
- output 8: float32 [1536, 1024], P('dp')
- output 9: float32 [1024, 1536], P('dp')
All inputs are finite; a program needn't handle non-finite values.
Results may differ from a plain program's by a relative error of at most 0.00113.
Values are sent between devices in bfloat16 or wider.
A program may use at most 1 GiB of HBM per device.

v0:
```python
import jax
import jax.numpy as jnp
from jax import lax
from jax.sharding import PartitionSpec as P

CAP_FACTOR = 2


def route_tables(ids_src, gates_src, buffer_pos, slot_cap):
    n_tok, n_top = ids_src.shape
    n_exp = buffer_pos.shape[0]
    hit_mask = ids_src[:, :, None] == jnp.arange(n_exp, dtype=ids_src.dtype)
    tok_hit = jnp.sum(hit_mask, axis=1, dtype=jnp.int32)
    rank_all = jnp.cumsum(tok_hit, axis=0) - tok_hit
    rank_pick = jnp.take_along_axis(rank_all, ids_src, axis=1)
    dest_slot = buffer_pos[ids_src] * slot_cap + rank_pick
    token_ids = jnp.broadcast_to(jnp.arange(n_tok, dtype=jnp.int32)[:, None], (n_tok, n_top))
    slot_token = jnp.full((n_exp * slot_cap,), n_tok, jnp.int32).at[dest_slot].set(token_ids)
    slot_gate = jnp.zeros((n_exp * slot_cap,), jnp.float32).at[dest_slot].set(gates_src)
    return dest_slot, slot_token, slot_gate


def take_rows(table_rows, row_ids):
    return jnp.take(table_rows, row_ids, axis=0, mode='fill', fill_value=0)


def silu_grad(pre_act):
    sigmoid_val = jax.nn.sigmoid(pre_act)
    return sigmoid_val * (1.0 + pre_act * (1.0 - sigmoid_val))


def exchange(buffer):
    moved_once = lax.all_to_all(buffer, 'eo', 2, 2)
    return lax.all_to_all(moved_once, 'ei', 1, 1)


def solution(mesh):
    ei_size = mesh.shape['ei']
    eo_size = mesh.shape['eo']
    group_size = ei_size * eo_size
    tok_spec = P(('dp', 'ei', 'eo'), None)
    exp_spec = P(('ei', 'eo'), None, None)
    full_spec = P(None, None)
    grad_spec = P(('dp', 'ei', 'eo'), None, None)
    shared_spec = P('dp', None)

    def device_step(x_loc, ids_loc, gates_loc, w_one, w_three, w_two, s_one, s_three, s_two, dy_loc):
        n_tok, n_top = ids_loc.shape
        model_dim = x_loc.shape[1]
        n_local = w_one.shape[0]
        n_exp = n_local * group_size
        slot_cap = min(n_tok, CAP_FACTOR * ((n_tok * n_top + n_exp - 1) // n_exp))
        expert_range = jnp.arange(n_exp, dtype=jnp.int32)
        buffer_pos = (expert_range % n_local) * group_size + expert_range // n_local
        dest_slot, slot_token, slot_gate = route_tables(ids_loc, gates_loc, buffer_pos, slot_cap)
        buf_shape = (n_local, ei_size, eo_size, slot_cap, model_dim)
        recv_shape = (n_local, group_size * slot_cap, model_dim)
        flat_shape = (n_exp * slot_cap, model_dim)
        recv_x = exchange(take_rows(x_loc, slot_token).reshape(buf_shape)).reshape(recv_shape)
        pre_one = jnp.einsum('erd,edf->erf', recv_x, w_one, preferred_element_type=jnp.float32)
        pre_three = jnp.einsum('erd,edf->erf', recv_x, w_three, preferred_element_type=jnp.float32)
        act_h = (jax.nn.silu(pre_one) * pre_three).astype(jnp.bfloat16)
        out_rows = jnp.einsum('erf,efd->erd', act_h, w_two, preferred_element_type=jnp.float32).astype(jnp.bfloat16)
        back_out = exchange(out_rows.reshape(buf_shape)).reshape(flat_shape)
        out_pick = jnp.take(back_out, dest_slot, axis=0)
        y_route = jnp.sum(out_pick * gates_loc[:, :, None], axis=1)
        d_gates = jnp.einsum('tjd,td->tj', out_pick, dy_loc, preferred_element_type=jnp.float32)
        sh_one = jnp.dot(x_loc, s_one, preferred_element_type=jnp.float32)
        sh_three = jnp.dot(x_loc, s_three, preferred_element_type=jnp.float32)
        sh_act = (jax.nn.silu(sh_one) * sh_three).astype(jnp.bfloat16)
        y_loc = (y_route + jnp.dot(sh_act, s_two, preferred_element_type=jnp.float32)).astype(jnp.bfloat16)
        send_do = (take_rows(dy_loc, slot_token) * slot_gate[:, None]).astype(jnp.bfloat16)
        recv_do = exchange(send_do.reshape(buf_shape)).reshape(recv_shape)
        grad_h = jnp.einsum('erd,efd->erf', recv_do, w_two, preferred_element_type=jnp.float32)
        da_one = (grad_h * pre_three * silu_grad(pre_one)).astype(jnp.bfloat16)
        da_three = (grad_h * jax.nn.silu(pre_one)).astype(jnp.bfloat16)
        dx_rows = (jnp.einsum('erf,edf->erd', da_one, w_one, preferred_element_type=jnp.float32) + jnp.einsum('erf,edf->erd', da_three, w_three, preferred_element_type=jnp.float32)).astype(jnp.bfloat16)
        back_dx = exchange(dx_rows.reshape(buf_shape)).reshape(flat_shape)
        dx_route = jnp.sum(jnp.take(back_dx, dest_slot, axis=0), axis=1, dtype=jnp.float32)
        dw_one = jnp.einsum('erd,erf->edf', recv_x, da_one, preferred_element_type=jnp.float32).astype(jnp.bfloat16)
        dw_three = jnp.einsum('erd,erf->edf', recv_x, da_three, preferred_element_type=jnp.float32).astype(jnp.bfloat16)
        dw_two = jnp.einsum('erf,erd->efd', act_h, recv_do, preferred_element_type=jnp.float32).astype(jnp.bfloat16)
        grad_sh = jnp.einsum('td,fd->tf', dy_loc, s_two, preferred_element_type=jnp.float32)
        ds_one = (grad_sh * sh_three * silu_grad(sh_one)).astype(jnp.bfloat16)
        ds_three = (grad_sh * jax.nn.silu(sh_one)).astype(jnp.bfloat16)
        dx_shared = jnp.einsum('tf,df->td', ds_one, s_one, preferred_element_type=jnp.float32) + jnp.einsum('tf,df->td', ds_three, s_three, preferred_element_type=jnp.float32)
        dx_loc = (dx_route + dx_shared).astype(jnp.bfloat16)
        dws_one = jnp.einsum('td,tf->df', x_loc, ds_one, preferred_element_type=jnp.float32)
        dws_three = jnp.einsum('td,tf->df', x_loc, ds_three, preferred_element_type=jnp.float32)
        dws_two = jnp.einsum('tf,td->fd', sh_act, dy_loc, preferred_element_type=jnp.float32)
        dws_one, dws_three, dws_two = lax.psum((dws_one, dws_three, dws_two), ('ei', 'eo'))
        return (y_loc, dx_loc, d_gates, dw_one, dw_three, dw_two, dws_one, dws_three, dws_two)

    return jax.shard_map(device_step, mesh=mesh, in_specs=(tok_spec, tok_spec, tok_spec, exp_spec, exp_spec, exp_spec, full_spec, full_spec, full_spec, tok_spec), out_specs=(tok_spec, tok_spec, tok_spec, grad_spec, grad_spec, grad_spec, shared_spec, shared_spec, shared_spec), check_vma=False)
```

profile of v0, /device:TPU:0, one launch (start us, length us, event | category | flops | bytes accessed | tf_op | source)
XLA Modules:
  0.0 8375.6 jit_solution(7874609835430337602)
XLA Ops:
  13.9 34.8 reduce-window.6
  58.9 228.1 %gather_fusion = s32[12288]{0:T(1024)S(1)} fusion(s32[2048,64]{0,1:T(8,128)} %fusion.5, s32[12288]{0:T(1024)S(1)} %reshape.193), kind=kCustom, calls=%fused_computation.4 | custom fusion | bytes 196608 | tf_op jit(solution)/shard_map/jit(take_along_axis)/gather | solution.py:15
  290.6 40.9 compare_and_fusion.1
  337.8 45.4 scatter_custom_fusion
  387.2 46.2 scatter_custom_fusion.1
  433.3 149.2 %gather_fusion.3 = bf16[24576,1536]{1,0:T(8,128)(2,1)} fusion(bf16[2048,1536]{1,0:T(8,128)(2,1)} %param.23, s32[24576]{0:T(1024)S(1)} %fusion.6), kind=kCustom, calls=%fused_computation.2.clone | custom fusion | bytes 151093248 | tf_op jit(solution)/shard_map/jit(_take)/gather | solution.py:24
  582.6 50.0 multiply_convert_fusion
  632.6 50.2 copy.112
  682.8 14.6 all-to-all-start.4
  697.4 149.2 %gather_fusion.1 = bf16[24576,1536]{1,0:T(8,128)(2,1)} fusion(bf16[2048,1536]{1,0:T(8,128)(2,1)} %param.14, s32[24576]{0:T(1024)S(1)} %fusion.6), kind=kCustom, calls=%fused_computation.clone | custom fusion | bytes 151093248 | tf_op jit(solution)/shard_map/jit(_take)/gather | solution.py:24
  846.6 49.3 broadcast_select_fusion
  895.9 50.2 copy.102
  946.1 559.4 %all-to-all-done.4 = bf16[8,2,4,384,1536]{4,3,1,0,2:T(8,128)(2,1)} async-done(((bf16[8,2,4,384,1536]{4,3,1,0,2:T(8,128)(2,1)}), bf16[8,2,4,384,1536]{4,3,1,0,2:T(8,128)(2,1)}, u32[]{:S(2)}, u32[]{:S(2)}) %all-to-all-start.4) | async-done | bytes 75497504 | tf_op jit(solution)/shard_map/all_to_all | solution.py:33
  1505.5 14.6 all-to-all-start
  1520.1 49.5 copy.113
  1569.7 761.6 %all-to-all-done = bf16[8,2,4,384,1536]{4,3,1,0,2:T(8,128)(2,1)} async-done(((bf16[8,2,4,384,1536]{4,3,1,0,2:T(8,128)(2,1)}), bf16[8,2,4,384,1536]{4,3,1,0,2:T(8,128)(2,1)}, u32[]{:S(2)}, u32[]{:S(2)}) %all-to-all-start) | async-done | bytes 75497504 | tf_op jit(solution)/shard_map/all_to_all | solution.py:33
  2331.3 26.6 all-to-all-start.5
  2357.9 50.3 copy.103
  2408.2 778.7 %all-to-all-done.5 = bf16[8,2,4,384,1536]{4,3,2,0,1:T(8,128)(2,1)} async-done(((bf16[8,2,4,384,1536]{4,3,2,0,1:T(8,128)(2,1)}), bf16[8,2,4,384,1536]{4,3,2,0,1:T(8,128)(2,1)}, u32[]{:S(2)}, u32[]{:S(2)}) %all-to-all-start.5) | async-done | bytes 75497504 | tf_op jit(solution)/shard_map/all_to_all | solution.py:34
  3187.0 26.8 all-to-all-start.1
  3213.8 50.2 copy.114
  3264.0 55.7 fusion.22
  3319.7 704.8 %all-to-all-done.1 = bf16[8,2,4,384,1536]{4,3,2,0,1:T(8,128)(2,1)} async-done(((bf16[8,2,4,384,1536]{4,3,2,0,1:T(8,128)(2,1)}), bf16[8,2,4,384,1536]{4,3,2,0,1:T(8,128)(2,1)}, u32[]{:S(2)}, u32[]{:S(2)}) %all-to-all-start.1) | async-done | bytes 75497504 | tf_op jit(solution)/shard_map/all_to_all | solution.py:34
  4024.5 50.2 copy.104
  4074.7 53.9 fusion.19
  4128.5 93.3 %multiply_convert_fusion.3 = (bf16[8,3072,512]{2,1,0:T(8,128)(2,1)}, bf16[8,3072,512]{2,1,0:T(8,128)(2,1)}, bf16[8,3072,512]{2,1,0:T(8,128)(2,1)}) fusion(f32[8,3072,512]{2,1,0:T(8,128)} %fusion.19, f32[8,3072,512]{2,1,0:T(8,128)} %fusion.22, bf16[8,3072,1536]{2,1,0:T(8,128)(2,1)} %bitcast.70, bf16[8,1536,512]{2,1,0:T(8,128)(2,1)} %param.18), kind=kOutput, calls=%fused_computation.15 | convolution fusion | flops 38843449344 | bytes 264241152 | tf_op jit(solution)/shard_map/erd,edf->erf/dot_general | solution.py:61
  4221.9 50.2 convolution_convert_fusion
  4272.1 50.2 copy.105
  4322.3 14.5 all-to-all-start.2
  4336.8 67.4 fusion.23
  4404.2 87.7 %add_convert_fusion = bf16[8,3072,1536]{2,1,0:T(8,128)(2,1)} fusion(f32[8,3072,1536]{2,1,0:T(8,128)} %fusion.23, bf16[8,3072,512]{2,1,0:T(8,128)(2,1)} %get-tuple-element.65, bf16[8,1536,512]{2,1,0:T(8,128)(2,1)} %param.18), kind=kOutput, calls=%fused_computation.7 | convolution fusion | flops 38730203136 | bytes 264241152 | tf_op jit(solution)/shard_map/erf,edf->erd/dot_general | solution.py:77
  4491.9 50.3 copy.115
  4542.3 606.5 %all-to-all-done.2 = bf16[8,2,4,384,1536]{4,3,1,0,2:T(8,128)(2,1)} async-done(((bf16[8,2,4,384,1536]{4,3,1,0,2:T(8,128)(2,1)}), bf16[8,2,4,384,1536]{4,3,1,0,2:T(8,128)(2,1)}, u32[]{:S(2)}, u32[]{:S(2)}) %all-to-all-start.2) | async-done | bytes 75497504 | tf_op jit(solution)/shard_map/all_to_all | solution.py:33
  5148.7 14.8 all-to-all-start.6
  5163.5 49.6 copy.106
  5213.1 762.3 %all-to-all-done.6 = bf16[8,2,4,384,1536]{4,3,1,0,2:T(8,128)(2,1)} async-done(((bf16[8,2,4,384,1536]{4,3,1,0,2:T(8,128)(2,1)}), bf16[8,2,4,384,1536]{4,3,1,0,2:T(8,128)(2,1)}, u32[]{:S(2)}, u32[]{:S(2)}) %all-to-all-start.6) | async-done | bytes 75497504 | tf_op jit(solution)/shard_map/all_to_all | solution.py:33
  5975.4 26.7 all-to-all-start.3
  6002.2 11.8 fusion.20
  6014.0 10.8 fusion.21
  6024.8 18.6 multiply_convert_fusion.4
  6043.4 12.2 convolution_bitcast_fusion
  6055.6 10.8 convolution_bitcast_fusion.1
  6066.4 8.8 fusion.25
  6075.2 50.2 copy.116
  6125.5 890.0 %all-to-all-done.3 = bf16[8,2,4,384,1536]{4,3,2,0,1:T(8,128)(2,1)} async-done(((bf16[8,2,4,384,1536]{4,3,2,0,1:T(8,128)(2,1)}), bf16[8,2,4,384,1536]{4,3,2,0,1:T(8,128)(2,1)}, u32[]{:S(2)}, u32[]{:S(2)}) %all-to-all-start.3) | async-done | bytes 75497504 | tf_op jit(solution)/shard_map/all_to_all | solution.py:34
  7015.5 26.6 all-to-all-start.7
  7043.8 12.8 fusion.24
  7056.6 6.6 copy.122
  7063.2 6.6 copy.123
  7069.7 50.1 convolution_convert_fusion.3
  7119.9 50.3 convolution_convert_fusion.2
  7170.2 51.2 convolution_convert_fusion.1
  7221.4 50.2 copy.107
  7271.6 262.6 %gather_fusion.2 = bf16[12288,1536]{1,0:T(8,128)(2,1)} fusion(bf16[24576,1536]{1,0:T(8,128)(2,1)} %bitcast.72, s32[12288]{0:T(1024)S(1)} %copy-done.1), kind=kCustom, calls=%fused_computation.1.clone | custom fusion | bytes 75546624 | tf_op jit(solution)/shard_map/jit(_take)/gather | solution.py:65
  7534.2 57.0 reshape.239
  7591.2 42.4 fusion.1
  7636.9 215.6 %all-to-all-done.7 = bf16[8,2,4,384,1536]{4,3,2,0,1:T(8,128)(2,1)} async-done(((bf16[8,2,4,384,1536]{4,3,2,0,1:T(8,128)(2,1)}), bf16[8,2,4,384,1536]{4,3,2,0,1:T(8,128)(2,1)}, u32[]{:S(2)}, u32[]{:S(2)}) %all-to-all-start.7) | async-done | bytes 75497504 | tf_op jit(solution)/shard_map/all_to_all | solution.py:34
  7852.5 50.3 copy.117
  7902.8 262.6 %gather_fusion.4 = bf16[12288,1536]{1,0:T(8,128)(2,1)} fusion(bf16[24576,1536]{1,0:T(8,128)(2,1)} %bitcast.76, s32[12288]{0:T(1024)S(1)} %copy-done.1), kind=kCustom, calls=%fused_computation.3.clone | custom fusion | bytes 75546624 | tf_op jit(solution)/shard_map/jit(_take)/gather | solution.py:79
  8165.4 57.0 reshape.245
  8222.4 112.2 %convert_reduce_fusion = (f32[2048,1536]{1,0:T(8,128)}, f32[2048,1536]{1,0:T(8,128)}) fusion(bf16[2048,6,1536]{2,1,0:T(8,128)(2,1)} %reshape.245, pred[2048,6]{1,0:T(8,128)(4,1)S(1)} %copy-done.4, f32[2048,6]{1,0:T(8,128)} %copy.109, bf16[2048,6,1536]{2,1,0:T(8,128)(2,1)} %reshape.239), kind=kLoop, calls=%fused_computation.9 | loop fusion | flops 125829120 | bytes 100724736 | tf_op jit(solution)/shard_map/reduce_sum | solution.py:79
  8334.6 13.0 add_convert_fusion.2
  8347.6 14.8 add_convert_fusion.1
  8362.4 5.9 copy.138
  (70 shorter events, 35.8 us)
Async XLA Ops:
  7.2 6017.6 %copy-start = (bf16[1024,1536]{1,0:T(8,128)(2,1)S(1)}, bf16[1024,1536]{1,0:T(8,128)(2,1)}, u32[]{:S(2)}) copy-start(bf16[1024,1536]{1,0:T(8,128)(2,1)} %param.22) | copy-start | bytes 9437188
  12.2 0.8 copy-start.2
  58.9 231.7 %copy-start.5 = (s32[2048,6]{0,1:T(8,128)S(1)}, s32[2048,6]{0,1:T(8,128)}, u32[]{:S(2)}) copy-start(s32[2048,6]{0,1:T(8,128)} %param.15) | copy-start | bytes 147460
  58.9 325.0 %copy-start.11 = (f32[2048,6]{0,1:T(8,128)S(1)}, f32[2048,6]{0,1:T(8,128)}, u32[]{:S(2)}) copy-start(f32[2048,6]{0,1:T(8,128)} %param.16) | copy-start | bytes 147460
  334.8 52.4 copy-start.9
  433.3 149.2 %copy-start.6 = (f32[24576]{0:T(1024)S(1)}, f32[24576]{0:T(1024)}, u32[]{:S(2)}) copy-start(f32[24576]{0:T(1024)} %scatter_custom_fusion.1) | copy-start | bytes 294916
  433.3 149.2 %copy-start.7 = (pred[24576]{0:T(1024)(128)(4,1)S(1)}, pred[24576]{0:T(1024)(128)(4,1)}, u32[]{:S(2)}) copy-start(pred[24576]{0:T(1024)(128)(4,1)} %compare_and_fusion) | copy-start | bytes 73732
  682.8 822.8 %all-to-all-start.4 = ((bf16[8,2,4,384,1536]{4,3,1,0,2:T(8,128)(2,1)}), bf16[8,2,4,384,1536]{4,3,1,0,2:T(8,128)(2,1)}, u32[]{:S(2)}, u32[]{:S(2)}) async-start(bf16[8,2,4,384,1536]{4,3,1,0,2:T(8,128)(2,1)} %copy.112), calls=%async_computation.4 | async-start | bytes 150994944 | tf_op jit(solution)/shard_map/all_to_all | solution.py:33
  697.3 149.2 %copy-start.8 = (pred[24576]{0:T(1024)(128)(4,1)S(1)}, pred[24576]{0:T(1024)(128)(4,1)}, u32[]{:S(2)}) copy-start(pred[24576]{0:T(1024)(128)(4,1)} %compare_and_fusion) | copy-start | bytes 73732
  1505.5 825.8 %all-to-all-start = ((bf16[8,2,4,384,1536]{4,3,1,0,2:T(8,128)(2,1)}), bf16[8,2,4,384,1536]{4,3,1,0,2:T(8,128)(2,1)}, u32[]{:S(2)}, u32[]{:S(2)}) async-start(bf16[8,2,4,384,1536]{4,3,1,0,2:T(8,128)(2,1)} %copy.102), calls=%async_computation | async-start | bytes 150994944 | tf_op jit(solution)/shard_map/all_to_all | solution.py:33
  2331.3 855.7 %all-to-all-start.5 = ((bf16[8,2,4,384,1536]{4,3,2,0,1:T(8,128)(2,1)}), bf16[8,2,4,384,1536]{4,3,2,0,1:T(8,128)(2,1)}, u32[]{:S(2)}, u32[]{:S(2)}) async-start(bf16[8,2,4,384,1536]{4,3,2,0,1:T(8,128)(2,1)} %copy.113), calls=%async_computation.5 | async-start | bytes 150994944 | tf_op jit(solution)/shard_map/all_to_all | solution.py:34
  3187.0 837.5 %all-to-all-start.1 = ((bf16[8,2,4,384,1536]{4,3,2,0,1:T(8,128)(2,1)}), bf16[8,2,4,384,1536]{4,3,2,0,1:T(8,128)(2,1)}, u32[]{:S(2)}, u32[]{:S(2)}) async-start(bf16[8,2,4,384,1536]{4,3,2,0,1:T(8,128)(2,1)} %copy.103), calls=%async_computation.1 | async-start | bytes 150994944 | tf_op jit(solution)/shard_map/all_to_all | solution.py:34
  4322.3 826.4 %all-to-all-start.2 = ((bf16[8,2,4,384,1536]{4,3,1,0,2:T(8,128)(2,1)}), bf16[8,2,4,384,1536]{4,3,1,0,2:T(8,128)(2,1)}, u32[]{:S(2)}, u32[]{:S(2)}) async-start(bf16[8,2,4,384,1536]{4,3,1,0,2:T(8,128)(2,1)} %copy.105), calls=%async_computation.2 | async-start | bytes 150994944 | tf_op jit(solution)/shard_map/all_to_all | solution.py:33
  5148.7 826.7 %all-to-all-start.6 = ((bf16[8,2,4,384,1536]{4,3,1,0,2:T(8,128)(2,1)}), bf16[8,2,4,384,1536]{4,3,1,0,2:T(8,128)(2,1)}, u32[]{:S(2)}, u32[]{:S(2)}) async-start(bf16[8,2,4,384,1536]{4,3,1,0,2:T(8,128)(2,1)} %copy.115), calls=%async_computation.6 | async-start | bytes 150994944 | tf_op jit(solution)/shard_map/all_to_all | solution.py:33
  5975.4 1040.1 %all-to-all-start.3 = ((bf16[8,2,4,384,1536]{4,3,2,0,1:T(8,128)(2,1)}), bf16[8,2,4,384,1536]{4,3,2,0,1:T(8,128)(2,1)}, u32[]{:S(2)}, u32[]{:S(2)}) async-start(bf16[8,2,4,384,1536]{4,3,2,0,1:T(8,128)(2,1)} %copy.106), calls=%async_computation.3 | async-start | bytes 150994944 | tf_op jit(solution)/shard_map/all_to_all | solution.py:34
  6002.1 1054.5 %all-reduce.3.cloned.1.call-start = ((), (), s32[]{:S(2)}) async-start(), calls=%async_computation.8 | async-start | bytes 37748736 | tf_op jit(solution)/shard_map/psum | solution.py:91
  6002.1 11.9 copy-start.13
  6043.4 12.2 copy-start.16
  6043.4 23.0 slice-start
  6055.6 10.8 slice-start.1
  6055.6 10.8 copy-start.15
  6125.5 916.6 %copy-start.12 = (pred[2048,6]{0,1:T(8,128)(4,1)S(1)}, pred[2048,6]{0,1:T(8,128)(4,1)}, u32[]{:S(2)}) copy-start(pred[2048,6]{0,1:T(8,128)(4,1)} %get-tuple-element.61) | copy-start | bytes 36868
  6125.5 917.7 %copy-start.10 = (s32[12288]{0:T(1024)S(1)}, s32[12288]{0:T(1024)}, u32[]{:S(2)}) copy-start(s32[12288]{0:T(1024)} %copy-done.9) | copy-start | bytes 147460
  7015.5 837.0 %all-to-all-start.7 = ((bf16[8,2,4,384,1536]{4,3,2,0,1:T(8,128)(2,1)}), bf16[8,2,4,384,1536]{4,3,2,0,1:T(8,128)(2,1)}, u32[]{:S(2)}, u32[]{:S(2)}) async-start(bf16[8,2,4,384,1536]{4,3,2,0,1:T(8,128)(2,1)} %copy.116), calls=%async_computation.7 | async-start | bytes 150994944 | tf_op jit(solution)/shard_map/all_to_all | solution.py:34
  7221.4 50.2 copy-start.1
  7534.2 57.0 copy-start.3
  8165.4 57.0 copy-start.4
  8334.6 13.0 copy-start.14
Sparse Core Ops, SparseCore 0:
  6075.4 431.6 all-reduce.2
where the time goes:
time: 8400 us; the launch traced here: 8380 us
  waiting for transfers between devices  5280 us (63%)
  local copies, waits for them, and re-layouts  1910 us (23%)
  matrix products  716 us (9%)
  other arithmetic  294 us (4%)
  starting transfers between devices  165 us (2%)
    all_to_all x4, waiting for transfers between devices, exchange(): moved_once = lax.all_to_all(buffer, 'eo', 2, 2)  2690 us
    all_to_all x4, waiting for transfers between devices, exchange(): return lax.all_to_all(moved_once, 'ei', 1, 1)  2590 us
    gather x2, local copies, waits for them, and re-layouts, device_step(): jnp.take(back_dx, dest_slot, axis=0)  320 us
    gather x2, local copies, waits for them, and re-layouts, device_step(): out_pick = jnp.take(back_out, dest_slot, axis=0)  320 us
    gather x2, local copies, waits for them, and re-layouts, take_rows(): return jnp.take(table_rows, row_ids, axis=0, mode='fill', fill_value=0)  298 us
    gather x5, local copies, waits for them, and re-layouts, route_tables(): rank_pick = jnp.take_along_axis(rank_all, ids_src, axis=1)  235 us
    all_to_all x4, local copies, waits for them, and re-layouts, exchange(): return lax.all_to_all(moved_once, 'ei', 1, 1)  201 us
    all_to_all x4, local copies, waits for them, and re-layouts, exchange(): moved_once = lax.all_to_all(buffer, 'eo', 2, 2)  200 us
  transfers between devices with their start and end apart: 9, of which 8 were waited for; matrix products, arithmetic and copies ran while one was open for 17% of the time, Pallas kernels for 0%

commit v1 on v0

v1 whole, which is shorter than its diff:
```python
import functools

import jax
import jax.numpy as jnp
from jax import lax
from jax.experimental import pallas as pl
from jax.experimental.pallas import tpu as pltpu
from jax.sharding import PartitionSpec as P

CAP_FACTOR = 2
CHUNKS = 4
BLK = 256
LANE = 128
SUB = 8
STAGE = 512
F32 = jnp.float32
BF16 = jnp.bfloat16


def silu_grad(pre_act):
    sigmoid_val = jax.nn.sigmoid(pre_act)
    return sigmoid_val * (1.0 + pre_act * (1.0 - sigmoid_val))


SMEM = pl.BlockSpec(memory_space=pltpu.SMEM)
HBM = pl.BlockSpec(memory_space=pl.ANY)
PARAMS = dict(vmem_limit_bytes=60 << 20)


def pipeline(body, n, in_specs=(), out_specs=()):
    return pltpu.emit_pipeline(lambda at, *refs: body(at.index[0], *refs), grid=(n,), in_specs=in_specs, out_specs=out_specs, _explicit_indices=True)


def gather_kernel(chunk_tok, dim, slot_cap, blk_e, blk_k, meta, slots, gsel, tok_hbm, *refs):
    x_out, dy_out, g_out, stage, rowbuf = refs[-5:]
    n_groups = dim // LANE
    off = meta[1]
    stage[chunk_tok // SUB] = jnp.zeros(stage.shape[1:], F32)

    def fill(step, tok_ref):
        def convert(i, carry):
            for c in range(n_groups):
                val = tok_ref[pl.ds(pl.multiple_of(i * 16, 16), 16), c * LANE:(c + 1) * LANE].astype(F32)
                at = step * (STAGE // SUB) + 2 * i
                stage[at, c * SUB:(c + 1) * SUB, :] = val[:SUB]
                stage[at + 1, c * SUB:(c + 1) * SUB, :] = val[SUB:]
            return carry
        lax.fori_loop(0, STAGE // 16, convert, 0)

    def rows(b, rows_ref, *gate):
        e = blk_e[b]
        base = e * slot_cap + blk_k[b] * BLK

        def move(g, carry):
            vals = []
            for r in range(SUB):
                t = slots[base + g * SUB + r]
                hi = t >> 3
                lo = t & 7
                vals.append((stage[hi, pl.ds(lo, 8, stride=SUB), :], stage[hi, pl.ds(lo + 64, n_groups - 8, stride=SUB), :]))
                if gate:
                    gate[0][g, r:r + 1, :] = jnp.full((1, LANE), gsel[e * chunk_tok + t], F32)
            for r in range(SUB):
                rowbuf[g, pl.ds(r, 8, stride=SUB), :] = vals[r][0]
                rowbuf[g, pl.ds(r + 64, n_groups - 8, stride=SUB), :] = vals[r][1]
            return carry
        lax.fori_loop(0, BLK // SUB, move, 0)

        def pack(i, carry):
            for c in range(n_groups):
                a = rowbuf[2 * i, c * SUB:(c + 1) * SUB, :]
                b2 = rowbuf[2 * i + 1, c * SUB:(c + 1) * SUB, :]
                rows_ref[pl.ds(pl.multiple_of(i * 16, 16), 16), c * LANE:(c + 1) * LANE] = jnp.concatenate([a, b2], axis=0).astype(BF16)
            return carry
        lax.fori_loop(0, BLK // 16, pack, 0)

    row_spec = pl.BlockSpec((BLK, dim), lambda i: (off + i, 0))
    gate_spec = pl.BlockSpec((BLK // SUB, SUB, LANE), lambda i: (off + i, 0, 0))
    n_stage = chunk_tok // STAGE
    pipeline(fill, n_stage, in_specs=[pl.BlockSpec((STAGE, dim), lambda i: (2 * i, 0))])(tok_hbm)
    pipeline(rows, meta[0], out_specs=[row_spec])(x_out)
    pipeline(fill, n_stage, in_specs=[pl.BlockSpec((STAGE, dim), lambda i: (2 * i + 1, 0))])(tok_hbm)
    pipeline(rows, meta[0], out_specs=[row_spec, gate_spec])(dy_out, g_out)


def gather_rows(tok, held, tables, n_rows):
    chunk_tok, dim = tok.shape[0] // 2, tok.shape[1]
    slot_cap = tables[3].shape[0] // 8
    return pl.pallas_call(
        functools.partial(gather_kernel, chunk_tok, dim, slot_cap),
        out_shape=[jax.ShapeDtypeStruct((n_rows, dim), BF16), jax.ShapeDtypeStruct((n_rows, dim), BF16),
                   jax.ShapeDtypeStruct((n_rows // SUB, SUB, LANE), F32)],
        in_specs=[SMEM] * 5 + [HBM] * (1 + len(held)),
        out_specs=[HBM] * 3,
        scratch_shapes=[pltpu.VMEM((chunk_tok // SUB + 1, dim // LANE * SUB, LANE), F32),
                        pltpu.VMEM((BLK // SUB, dim // LANE * SUB, LANE), F32)],
        input_output_aliases={6 + i: i for i in range(len(held))},
        compiler_params=pltpu.CompilerParams(**PARAMS),
        cost_estimate=pl.CostEstimate(flops=60_000_000_000, bytes_accessed=120_000_000, transcendentals=0),
        name="gather_rows",
    )(*tables, tok, *held)


def scale_rows(gate, dy):
    return jnp.concatenate([(gate * dy[:, c * LANE:(c + 1) * LANE]).astype(BF16) for c in range(dy.shape[1] // LANE)], axis=1)


def expert_body(e, x_ref, dy_ref, g_ref, w1_ref, w3_ref, w2_ref, o_ref, dx_ref, dg_ref, h_ref, d1_ref, d3_ref):
    x = x_ref[...]
    dot = functools.partial(jnp.dot, preferred_element_type=F32)
    dot_t = lambda a, b: lax.dot_general(a, b, (((1,), (1,)), ((), ())), preferred_element_type=F32)
    a1 = dot(x, w1_ref[0])
    a3 = dot(x, w3_ref[0])
    sig = jax.nn.sigmoid(a1)
    act = a1 * sig
    h = (act * a3).astype(BF16)
    h_ref[...] = h
    o = dot(h, w2_ref[0]).astype(BF16)
    o_ref[...] = o
    dy = dy_ref[...].astype(F32)
    prod = dy * o.astype(F32)
    part = prod[:, 0:LANE]
    for c in range(1, prod.shape[1] // LANE):
        part = part + prod[:, c * LANE:(c + 1) * LANE]
    dg = jnp.sum(part, axis=1, keepdims=True)
    lane = lax.broadcasted_iota(jnp.int32, part.shape, 1)
    dg_ref[...] = jnp.where(lane == e, dg, 0.0)
    dh = dot_t(scale_rows(g_ref[...], dy), w2_ref[0])
    d1 = (dh * a3 * (sig * (1.0 + a1 * (1.0 - sig)))).astype(BF16)
    d3 = (dh * act).astype(BF16)
    d1_ref[...] = d1
    d3_ref[...] = d3
    dx_ref[...] = (dot_t(d1, w1_ref[0]) + dot_t(d3, w3_ref[0])).astype(BF16)


def expert_kernel(blk_e, meta, x, dy, g, w1, w3, w2, *refs):
    outs = refs[-6:]
    dim, ffn = w1.shape[1:]
    off = meta[1]
    glob = lambda i: (off + i, 0)
    loc = lambda i: (i, 0)
    wmap = lambda i: (blk_e[i], 0, 0)
    pipeline(
        lambda b, *refs: expert_body(blk_e[b], *refs), meta[0],
        in_specs=[pl.BlockSpec((BLK, dim), glob), pl.BlockSpec((BLK, dim), glob), pl.BlockSpec((BLK, LANE), glob),
                  pl.BlockSpec((1, dim, ffn), wmap), pl.BlockSpec((1, dim, ffn), wmap), pl.BlockSpec((1, ffn, dim), wmap)],
        out_specs=[pl.BlockSpec((BLK, dim), loc), pl.BlockSpec((BLK, dim), loc), pl.BlockSpec((BLK, LANE), loc)]
        + [pl.BlockSpec((BLK, ffn), glob)] * 3)(x, dy, g, w1, w3, w2, *outs)


def run_experts(x_rows, dy_rows, gates, w1, w3, w2, saved, blk_e, meta):
    n_rows, dim = x_rows.shape
    loc_rows = blk_e.shape[0] * BLK
    return pl.pallas_call(
        expert_kernel,
        out_shape=[jax.ShapeDtypeStruct((loc_rows, dim), BF16), jax.ShapeDtypeStruct((loc_rows, dim), BF16),
                   jax.ShapeDtypeStruct((loc_rows, LANE), F32)] + [jax.ShapeDtypeStruct((n_rows, w1.shape[2]), BF16)] * 3,
        in_specs=[SMEM] * 2 + [HBM] * (6 + len(saved)),
        out_specs=[HBM] * 6,
        input_output_aliases={8 + i: 3 + i for i in range(len(saved))},
        compiler_params=pltpu.CompilerParams(**PARAMS),
        cost_estimate=pl.CostEstimate(flops=60_000_000_000, bytes_accessed=80_000_000, transcendentals=0),
        name="experts",
    )(blk_e, meta, x_rows, dy_rows, gates, w1, w3, w2, *saved)


def combine_kernel(n_groups, slot_cap, blk_e, blk_k, meta, slots, o_hbm, g_hbm, dg_hbm, dx_hbm, out_ref, dgo_ref, stage_y, stage_dx, rowbuf, sem):
    n_tiles = out_ref.shape[0]
    dim = n_groups * LANE
    used = n_groups * SUB
    off = meta[1]

    def rows(stage, planes, b, rows_ref, *gate):
        base = blk_e[b] * slot_cap + blk_k[b] * BLK

        def unpack(i, carry):
            if gate:
                ga = gate[0][2 * i]
                gb = gate[0][2 * i + 1]
            for c in range(n_groups):
                val = rows_ref[pl.ds(pl.multiple_of(i * 16, 16), 16), c * LANE:(c + 1) * LANE].astype(F32)
                lo, hi = val[:SUB], val[SUB:]
                if gate:
                    lo, hi = lo * ga, hi * gb
                rowbuf[2 * i, c * SUB:(c + 1) * SUB, :] = lo
                rowbuf[2 * i + 1, c * SUB:(c + 1) * SUB, :] = hi
            if gate:
                rowbuf[2 * i, used:, :] = gate[1][2 * i]
                rowbuf[2 * i + 1, used:, :] = gate[1][2 * i + 1]
            return carry
        lax.fori_loop(0, BLK // 16, unpack, 0)

        def add(g, carry):
            todo = []
            for r in range(SUB):
                t = slots[base + g * SUB + r]
                hi = t >> 3
                lo = t & 7
                a = stage[hi, pl.ds(lo, 8, stride=SUB), :] + rowbuf[g, pl.ds(r, 8, stride=SUB), :]
                c = stage[hi, pl.ds(lo + 64, planes - 8, stride=SUB), :] + rowbuf[g, pl.ds(r + 64, planes - 8, stride=SUB), :]
                todo.append((hi, lo, a, c))
            for hi, lo, a, c in todo:
                stage[hi, pl.ds(lo, 8, stride=SUB), :] = a
                stage[hi, pl.ds(lo + 64, planes - 8, stride=SUB), :] = c
            return carry
        lax.fori_loop(0, BLK // SUB, add, 0)

    def clear(stage):
        def zero(i, carry):
            stage[i] = jnp.zeros(stage.shape[1:], F32)
            return carry
        lax.fori_loop(0, n_tiles + 1, zero, 0)

    row_spec = pl.BlockSpec((BLK, dim), lambda i: (i, 0))
    gate_spec = pl.BlockSpec((BLK // SUB, SUB, LANE), lambda i: (off + i, 0, 0))
    dg_spec = pl.BlockSpec((BLK // SUB, SUB, LANE), lambda i: (i, 0, 0))
    tiles = pl.ds(0, n_tiles)
    copies = [pltpu.make_async_copy(stage_y.at[tiles, pl.ds(0, used)], out_ref.at[:, pl.ds(0, used)], sem.at[0]),
              pltpu.make_async_copy(stage_y.at[tiles, pl.ds(used, SUB)], dgo_ref, sem.at[1]),
              pltpu.make_async_copy(stage_dx.at[tiles], out_ref.at[:, pl.ds(used, used)], sem.at[2])]
    clear(stage_y)
    pipeline(functools.partial(rows, stage_y, n_groups + 1), meta[0], in_specs=[row_spec, gate_spec, dg_spec])(o_hbm, g_hbm, dg_hbm)
    copies[0].start()
    copies[1].start()
    clear(stage_dx)
    pipeline(functools.partial(rows, stage_dx, n_groups), meta[0], in_specs=[row_spec])(dx_hbm)
    copies[2].start()
    for copy in copies:
        copy.wait()


def combine_rows(o_rows, gates, dg, dx_rows, tables, chunk_tok):
    n_groups = o_rows.shape[1] // LANE
    slot_cap = tables[3].shape[0] // 8
    n_tiles = chunk_tok // SUB
    return pl.pallas_call(
        functools.partial(combine_kernel, n_groups, slot_cap),
        out_shape=[jax.ShapeDtypeStruct((n_tiles, 2 * n_groups * SUB, LANE), F32), jax.ShapeDtypeStruct((n_tiles, SUB, LANE), F32)],
        in_specs=[SMEM] * 4 + [HBM] * 4,
        out_specs=[HBM] * 2,
        scratch_shapes=[pltpu.VMEM((n_tiles + 1, (n_groups + 1) * SUB, LANE), F32), pltpu.VMEM((n_tiles + 1, n_groups * SUB, LANE), F32),
                        pltpu.VMEM((BLK // SUB, (n_groups + 1) * SUB, LANE), F32), pltpu.SemaphoreType.DMA((3,))],
        compiler_params=pltpu.CompilerParams(**PARAMS),
        cost_estimate=pl.CostEstimate(flops=80_000_000_000, bytes_accessed=120_000_000, transcendentals=0),
        name="combine_rows",
    )(*tables[:4], o_rows, gates, dg, dx_rows)


def grad_kernel(order, owner, total, x, dy, g, h, d1, d3, o1, o3, o2, acc1, acc3, acc2):
    dim, ffn = o1.shape[1:]
    n = total[0]

    def step(i, x_ref, dy_ref, g_ref, h_ref, d1_ref, d3_ref, o1_ref, o3_ref, o2_ref):
        e = owner[i]
        first = jnp.logical_or(i == 0, owner[jnp.maximum(i - 1, 0)] != e)
        last = jnp.logical_or(i == n - 1, owner[jnp.minimum(i + 1, owner.shape[0] - 1)] != e)

        @pl.when(first)
        def _():
            acc1[...] = jnp.zeros_like(acc1)
            acc3[...] = jnp.zeros_like(acc3)
            acc2[...] = jnp.zeros_like(acc2)

        dot_l = lambda a, b: lax.dot_general(a, b, (((0,), (0,)), ((), ())), preferred_element_type=F32)
        x = x_ref[...]
        acc1[...] += dot_l(x, d1_ref[...])
        acc3[...] += dot_l(x, d3_ref[...])
        acc2[...] += dot_l(h_ref[...], scale_rows(g_ref[...], dy_ref[...].astype(F32)))

        @pl.when(last)
        def _():
            o1_ref[0] = acc1[...].astype(BF16)
            o3_ref[0] = acc3[...].astype(BF16)
            o2_ref[0] = acc2[...].astype(BF16)
    row = lambda i: (order[i], 0)
    wmap = lambda i: (owner[i], 0, 0)
    pipeline(
        step, n,
        in_specs=[pl.BlockSpec((BLK, dim), row), pl.BlockSpec((BLK, dim), row), pl.BlockSpec((BLK, LANE), row)]
        + [pl.BlockSpec((BLK, ffn), row)] * 3,
        out_specs=[pl.BlockSpec((1, dim, ffn), wmap), pl.BlockSpec((1, dim, ffn), wmap), pl.BlockSpec((1, ffn, dim), wmap)],
    )(x, dy, g, h, d1, d3, o1, o3, o2)


def weight_grads(x_rows, dy_rows, gates, saved, order, owner, total, n_local):
    dim = x_rows.shape[1]
    ffn = saved[0].shape[1]
    return pl.pallas_call(
        grad_kernel,
        out_shape=[jax.ShapeDtypeStruct((n_local, dim, ffn), BF16), jax.ShapeDtypeStruct((n_local, dim, ffn), BF16),
                   jax.ShapeDtypeStruct((n_local, ffn, dim), BF16)],
        in_specs=[SMEM] * 3 + [HBM] * 6,
        out_specs=[HBM] * 3,
        scratch_shapes=[pltpu.VMEM((dim, ffn), F32), pltpu.VMEM((dim, ffn), F32), pltpu.VMEM((ffn, dim), F32)],
        compiler_params=pltpu.CompilerParams(**PARAMS),
        cost_estimate=pl.CostEstimate(flops=100_000_000_000, bytes_accessed=160_000_000, transcendentals=0),
        name="weight_grads",
    )(order, owner, total, x_rows, dy_rows, gates, *saved)


def route(ids_all, gates_all, first_expert, n_local, slot_cap):
    n_chunk, n_top, chunk_tok = ids_all.shape
    experts = first_expert + jnp.arange(n_local, dtype=jnp.int32)
    match = ids_all[:, None] == experts[None, :, None, None]
    hit = jnp.any(match, axis=2)
    gsel = jnp.sum(jnp.where(match, gates_all[:, None], 0.0), axis=2)
    n_seg = chunk_tok // LANE
    strict = (jnp.arange(LANE)[:, None] < jnp.arange(LANE)[None, :]).astype(BF16)
    seg = hit.reshape(n_chunk, n_local, n_seg, LANE)
    inner = jnp.einsum('cesl,lm->cesm', seg.astype(BF16), strict, preferred_element_type=F32)
    seg_sum = jnp.sum(seg, axis=3, dtype=jnp.int32)
    before = jnp.arange(n_seg)[:, None] < jnp.arange(n_seg)[None, :]
    outer = jnp.sum(jnp.where(before, seg_sum[..., :, None], 0), axis=2)
    rank = (inner.astype(jnp.int32) + outer[..., None]).reshape(n_chunk, n_local, chunk_tok)
    count = jnp.sum(seg_sum, axis=2)
    n_hi = slot_cap // 64
    hi = jnp.where(hit, rank >> 6, -1)
    lo = rank & 63
    pick_hi = (hi[:, :, None, :] == jnp.arange(n_hi, dtype=jnp.int32)[:, None]).astype(BF16)
    tok = jnp.arange(chunk_tok, dtype=jnp.int32)
    pick_lo = lo[:, :, None, :] == jnp.arange(64, dtype=jnp.int32)[:, None]
    val_lo = jnp.concatenate([jnp.where(pick_lo, (tok >> 6), 0), jnp.where(pick_lo, (tok & 63), 0)], axis=2).astype(BF16)
    found = jnp.einsum('ceht,cent->cehn', pick_hi, val_lo, preferred_element_type=F32).astype(jnp.int32)
    slots = (found[..., :64] * 64 + found[..., 64:]).reshape(n_chunk, n_local, slot_cap)
    slots = jnp.where(jnp.arange(slot_cap, dtype=jnp.int32) < count[..., None], slots, chunk_tok)
    n_blk = (count + BLK - 1) // BLK
    upto = jnp.cumsum(n_blk, axis=1)
    chunk_blk = upto[:, -1]
    chunk_off = jnp.cumsum(chunk_blk) - chunk_blk
    max_blk = n_local * (slot_cap // BLK)
    at = jnp.arange(max_blk, dtype=jnp.int32)
    blk_e = jnp.minimum(jnp.sum(at[None, :, None] >= upto[:, None, :], axis=2, dtype=jnp.int32), n_local - 1)
    start = upto - n_blk
    blk_k = at[None, :] - jnp.sum(jnp.where(blk_e[..., None] == jnp.arange(n_local), start[:, None, :], 0), axis=2)
    glob = (chunk_off[:, None] + start).T.reshape(-1)
    cnt = n_blk.T.reshape(-1)
    end = jnp.cumsum(cnt)
    total_blk = end[-1]
    at2 = jnp.arange(n_local * slot_cap // BLK + n_chunk * n_local, dtype=jnp.int32)
    grp = jnp.minimum(jnp.sum(at2[:, None] >= end[None, :], axis=1, dtype=jnp.int32), cnt.shape[0] - 1)
    sel = grp[:, None] == jnp.arange(cnt.shape[0])
    order = at2 + jnp.sum(jnp.where(sel, (glob - (end - cnt))[None, :], 0), axis=1)
    order = jnp.clip(order, 0, at2.shape[0] - 1).astype(jnp.int32)
    owner = (grp // n_chunk).astype(jnp.int32)
    return slots, gsel, blk_e, blk_k.astype(jnp.int32), chunk_blk, chunk_off, order, owner, total_blk


def solution(mesh):
    ei_size = mesh.shape['ei']
    eo_size = mesh.shape['eo']
    group_size = ei_size * eo_size
    axes = ('ei', 'eo')
    tok_spec = P(('dp', 'ei', 'eo'), None)
    exp_spec = P(('ei', 'eo'), None, None)
    full_spec = P(None, None)
    grad_spec = P(('dp', 'ei', 'eo'), None, None)
    shared_spec = P('dp', None)

    def device_step(x_loc, ids_loc, gates_loc, w_one, w_three, w_two, s_one, s_three, s_two, dy_loc):
        n_tok, n_top = ids_loc.shape
        dim = x_loc.shape[1]
        ffn = w_one.shape[2]
        n_local = w_one.shape[0]
        n_exp = n_local * group_size
        cap = min(n_tok, CAP_FACTOR * ((n_tok * n_top + n_exp - 1) // n_exp))
        slot_cap = cap * group_size
        part = n_tok // CHUNKS
        chunk_tok = part * group_size
        me = lax.axis_index('ei') * eo_size + lax.axis_index('eo')

        ids_t = lax.all_gather(ids_loc.T, axes, axis=0)
        gates_t = lax.all_gather(gates_loc.T, axes, axis=0)
        split = lambda v: v.reshape(group_size, n_top, CHUNKS, part).transpose(2, 1, 0, 3).reshape(CHUNKS, n_top, chunk_tok)
        tok_chunks = [lax.all_gather(jnp.concatenate([v[c * part:(c + 1) * part] for v in (x_loc, dy_loc)]), axes, axis=0, tiled=True) for c in range(CHUNKS)]
        slots, gsel, blk_e, blk_k, chunk_blk, chunk_off, order, owner, total_blk = route(
            split(ids_t), split(gates_t), me * n_local, n_local, slot_cap)
        n_rows = order.shape[0] * BLK

        sh_one = jnp.dot(x_loc, s_one, preferred_element_type=F32)
        sh_three = jnp.dot(x_loc, s_three, preferred_element_type=F32)
        sh_act = (jax.nn.silu(sh_one) * sh_three).astype(BF16)
        y_shared = jnp.dot(sh_act, s_two, preferred_element_type=F32)
        grad_sh = jnp.einsum('td,fd->tf', dy_loc, s_two, preferred_element_type=F32)
        ds_one = (grad_sh * sh_three * silu_grad(sh_one)).astype(BF16)
        ds_three = (grad_sh * jax.nn.silu(sh_one)).astype(BF16)
        dx_shared = jnp.einsum('tf,df->td', ds_one, s_one, preferred_element_type=F32) + jnp.einsum('tf,df->td', ds_three, s_three, preferred_element_type=F32)
        dws_one = jnp.einsum('td,tf->df', x_loc, ds_one, preferred_element_type=F32)
        dws_three = jnp.einsum('td,tf->df', x_loc, ds_three, preferred_element_type=F32)
        dws_two = jnp.einsum('tf,td->fd', sh_act, dy_loc, preferred_element_type=F32)

        held, saved = [], []
        sums, dg_parts = [], []
        for c in range(CHUNKS):
            meta = jnp.stack([chunk_blk[c], chunk_off[c]]).astype(jnp.int32)
            gpad = jnp.concatenate([gsel[c].reshape(-1), jnp.zeros((LANE,), F32)])
            tables = (blk_e[c], blk_k[c], meta, slots[c].reshape(-1), gpad)
            x_rows, dy_rows, gate_rows = gather_rows(tok_chunks[c], held, tables, n_rows)
            o_rows, dx_rows, dg, *saved = run_experts(x_rows, dy_rows, gate_rows.reshape(n_rows, LANE), w_one, w_three, w_two, saved, blk_e[c], meta)
            part_sum, dg_part = combine_rows(o_rows, gate_rows, dg.reshape(-1, SUB, LANE), dx_rows, tables, chunk_tok)
            x_rows, part_sum = lax.optimization_barrier((x_rows, part_sum))
            held = [x_rows, dy_rows, gate_rows]
            sums.append(lax.psum_scatter(part_sum, axes, scatter_dimension=0, tiled=True))
            dg_parts.append(dg_part.reshape(group_size, part, LANE)[:, :, :n_local])
        dw_one, dw_three, dw_two = weight_grads(x_rows, dy_rows, gate_rows.reshape(n_rows, LANE), saved, order, owner, total_blk[None], n_local)

        n_groups = dim // LANE
        natural = lambda v: v.reshape(part // SUB, n_groups, SUB, LANE).transpose(0, 2, 1, 3).reshape(part, dim)
        y_loc = (jnp.concatenate([natural(v[:, :n_groups * SUB]) for v in sums]) + y_shared).astype(BF16)
        dx_loc = (jnp.concatenate([natural(v[:, n_groups * SUB:]) for v in sums]) + dx_shared).astype(BF16)
        dg_send = jnp.stack(dg_parts, axis=1)
        dg_recv = lax.all_to_all(dg_send, axes, 0, 0)
        dg_tok = dg_recv.transpose(1, 2, 0, 3).reshape(n_tok, n_exp)
        pick = ids_loc[:, :, None] == jnp.arange(n_exp, dtype=jnp.int32)
        d_gates = jnp.sum(jnp.where(pick, dg_tok[:, None, :], 0.0), axis=2)
        dws_one, dws_three, dws_two = lax.psum((dws_one, dws_three, dws_two), axes)
        return (y_loc, dx_loc, d_gates, dw_one, dw_three, dw_two, dws_one, dws_three, dws_two)

    return jax.shard_map(device_step, mesh=mesh, in_specs=(tok_spec, tok_spec, tok_spec, exp_spec, exp_spec, exp_spec, full_spec, full_spec, full_spec, tok_spec), out_specs=(tok_spec, tok_spec, tok_spec, grad_spec, grad_spec, grad_spec, shared_spec, shared_spec, shared_spec), check_vma=False)
```

time: 8400 us -> 1910 us (0.23)
  waiting for transfers between devices: 5280 us -> 670 us
  local copies, waits for them, and re-layouts: 1910 us -> 98.8 us
  Pallas kernels: 0 us -> 861 us
  matrix products: 716 us -> 131 us
  other arithmetic: 294 us -> 50 us
  starting transfers between devices: 165 us -> 44.6 us
    all_to_all x8 -> x1, waiting for transfers between devices: 5280 us -> 0.01 us  [device_step(): dg_recv = lax.all_to_all(dg_send, axes, 0, 0)]
    gather x15 -> x0, local copies, waits for them, and re-layouts: 1180 us -> none  [the longest x2 320 us: device_step(): jnp.take(back_dx, dest_slot, axis=0)]
    pallas_call x0 -> x13, Pallas kernels: none -> 861 us  [the longest x4 274 us: combine_rows(): pl.pallas_call(functools.partial(combine_kernel, n_groups, slot_cap), out...]
    reduce_scatter x0 -> x4, waiting for transfers between devices: none -> 670 us  [device_step(): lax.psum_scatter(part_sum, axes, scatter_dimension=0, tiled=True)]
    dot_general x19 -> x11, matrix products: 716 us -> 131 us  [the longest x1 18.5 us: device_step(): grad_sh = jnp.einsum('td,fd->tf', dy_loc, s_two, preferred_element_type=F32)]
    all_to_all x8 -> x0, local copies, waits for them, and re-layouts: 401 us -> none  [the longest x4 201 us: exchange(): return lax.all_to_all(moved_once, 'ei', 1, 1)]
    reshape x4 -> x11, local copies, waits for them, and re-layouts: 201 us -> 28 us  [the longest x4 23.8 us: device_step(): v.reshape(part // SUB, n_groups, SUB, LANE).transpose(0, 2, 1, 3)]
    all_to_all x8 -> x1, starting transfers between devices: 165 us -> 44.2 us  [device_step(): dg_recv = lax.all_to_all(dg_send, axes, 0, 0)]
  transfers between devices with their start and end apart: 9 -> 10, of which waited for: 8 -> 3; matrix products, arithmetic and copies ran while one was open for 17% -> 12% of each run, Pallas kernels for 0% -> 45%
where the time goes in v1:
time: 1910 us; the launch traced here: 1900 us
  Pallas kernels  861 us (45%)
  waiting for transfers between devices  670 us (35%)
  matrix products  131 us (7%)
  local copies, waits for them, and re-layouts  98.8 us (5%)
  other arithmetic  50 us (3%)
  starting transfers between devices  44.6 us (2%)
  blocking collectives  31.9 us (2%)
    reduce_scatter x4, waiting for transfers between devices, device_step(): lax.psum_scatter(part_sum, axes, scatter_dimension=0, tiled=True)  670 us
    pallas_call x4, Pallas kernels, combine_rows(): pl.pallas_call(functools.partial(combine_kernel, n_groups, slot_cap), out...  274 us
    pallas_call x4, Pallas kernels, gather_rows(): pl.pallas_call(functools.partial(gather_kernel, chunk_tok, dim, slot_cap)...  241 us
    pallas_call x4, Pallas kernels, run_experts(): pl.pallas_call(expert_kernel, out_shape=[jax.ShapeDtypeStruct((loc_rows,...  225 us
    pallas_call x1, Pallas kernels, weight_grads(): pl.pallas_call(grad_kernel, out_shape=[jax.ShapeDtypeStruct((n_local, dim...  121 us
    all_to_all x1, starting transfers between devices, device_step(): dg_recv = lax.all_to_all(dg_send, axes, 0, 0)  44.2 us
  transfers between devices with their start and end apart: 10, of which 3 were waited for; matrix products, arithmetic and copies ran while one was open for 12% of the time, Pallas kernels for 45%

profile of v1, /device:TPU:0, one launch (start us, length us, event | category | flops | bytes accessed | tf_op | source)
XLA Modules:
  0.0 1902.8 jit_solution(12608425623479944701)
XLA Ops:
  7.2 8.7 fusion.25
  15.9 1.9 pad_maximum_fusion
  17.9 3.8 pad_maximum_fusion.1
  21.8 3.7 pad_maximum_fusion.2
  25.6 3.7 pad_maximum_fusion.3
  29.4 11.8 fusion.29
  41.3 10.8 fusion.30
  52.1 18.5 multiply_convert_fusion
  70.6 12.2 convolution_bitcast_fusion
  82.8 10.8 convolution_bitcast_fusion.1
  93.6 8.8 fusion.32
  103.3 19.0 %all-gather.2 = s32[8,6,2048]{2,1,0:T(8,128)} all-gather(s32[1,6,2048]{2,1,0:T(8,128)S(1)} %bitcast.218), channel_id=2, replica_groups=mesh['dp'=1,'ei'=2,'eo'=4] {'ei','eo'}, dimensions={0}, use_global_device_ids=true | all-gather | bytes 442368 | tf_op jit(solution)/shard_map/all_gather | solution.py:371
  122.3 1.3 reshape.260
  125.3 2.2 convert_reduce_fusion
  129.1 2.0 shift_right_arithmetic.21
  131.0 2.0 broadcast_select_fusion
  134.7 12.8 all-gather.3
  147.5 1.3 reshape.261
  149.1 1.5 fusion.8
  154.8 1.9 and.48
  156.8 14.3 select_convert_fusion.1
  171.1 15.7 fusion.9
  188.0 1.4 reshape.216
  190.9 1.6 concatenate.35.gsel
  192.4 1.9 pad_add_fusion.meta
  194.3 60.8 %gather_rows.4 = (bf16[32768,1536]{1,0:T(8,128)(2,1)}, bf16[32768,1536]{1,0:T(8,128)(2,1)}, f32[4096,8,128]{2,1,0:T(8,128)}) custom-call(s32[96]{0:T(128)} %get-tuple-element.240.blk_e, s32[96]{0:T(128)} %get-tuple-element.221.blk_k, s32[2]{0:T(128)} %pad_add_fusion.meta, s32[24576]{0:T(1024)} %bitcast.219, f32[32896]{0:T(1024)} %concatenate.35.gsel, ...), custom_call_target="tpu_custom_call" | custom-call | flops 60000002048 | bytes 120000000 | tf_op jit(solution)/shard_map/gather_rows/pallas_call | solution.py:89
  255.1 57.3 %experts.4 = (bf16[24576,1536]{1,0:T(8,128)(2,1)}, bf16[24576,1536]{1,0:T(8,128)(2,1)}, f32[24576,128]{1,0:T(8,128)}, bf16[32768,512]{1,0:T(8,128)(2,1)}, bf16[3...) custom-call(s32[96]{0:T(128)} %get-tuple-element.240.blk_e, s32[2]{0:T(128)} %pad_add_fusion.meta, ...), custom_call_target="tpu_custom_call" | custom-call | flops 60000002048 | bytes 80000000 | tf_op jit(solution)/shard_map/experts/pallas_call | solution.py:154
  312.5 69.1 %combine_rows.4 = (f32[512,192,128]{2,1,0:T(8,128)}, f32[512,8,128]{2,1,0:T(8,128)}) custom-call(s32[96]{0:T(128)} %get-tuple-element.240.blk_e, s32[96]{0:T(128)} %get-tuple-element.221.blk_k, s32[2]{0:T(128)} %pad_add_fusion.meta, s32[24576]{0:T(1024)} %bitcast.220, bf16[24576,1536]{1,0:T(8,128)(2,1)} %get-tuple-element.67.o_hbm, ...), custom_call_target="tpu_custom_call" | custom-call | flops 80000000000 | bytes 120000000 | tf_op jit(solution)/shard_map/combine_rows/pallas_call | solution.py:236
  383.8 1.8 pad_add_fusion.1.meta
  385.6 63.5 %gather_rows.5 = (bf16[32768,1536]{1,0:T(8,128)(2,1)}, bf16[32768,1536]{1,0:T(8,128)(2,1)}, f32[4096,8,128]{2,1,0:T(8,128)}) custom-call(s32[96]{0:T(128)} %get-tuple-element.237.blk_e, s32[96]{0:T(128)} %get-tuple-element.224.blk_k, s32[2]{0:T(128)} %pad_add_fusion.1.meta, ...), custom_call_target="tpu_custom_call", output_to_operand_aliasing={{0}: (6, {}), {1}: (7, {}), {2}: (8, {})} | custom-call | flops 60000002048 | bytes 120000000 | tf_op jit(solution)/shard_map/gather_rows/pallas_call | solution.py:89
  449.0 60.3 %experts.5 = (bf16[24576,1536]{1,0:T(8,128)(2,1)}, bf16[24576,1536]{1,0:T(8,128)(2,1)}, f32[24576,128]{1,0:T(8,128)}, bf16[32768,512]{1,0:T(8,128)(2,1)}, bf16[3...) custom-call(s32[96]{0:T(128)} %get-tuple-element.237.blk_e, ...), custom_call_target="tpu_custom_call", output_to_operand_aliasing={{3}: (8, {}), {4}: (9, {}), {5}: (10, {})} | custom-call | flops 60000002048 | bytes 80000000 | tf_op jit(solution)/shard_map/experts/pallas_call | solution.py:154
  509.4 72.3 %combine_rows.5 = (f32[512,192,128]{2,1,0:T(8,128)}, f32[512,8,128]{2,1,0:T(8,128)}) custom-call(s32[96]{0:T(128)} %get-tuple-element.237.blk_e, s32[96]{0:T(128)} %get-tuple-element.224.blk_k, s32[2]{0:T(128)} %pad_add_fusion.1.meta, s32[24576]{0:T(1024)} %bitcast.215, bf16[24576,1536]{1,0:T(8,128)(2,1)} %get-tuple-element.79.o_hbm, ...), custom_call_target="tpu_custom_call" | custom-call | flops 80000000000 | bytes 120000000 | tf_op jit(solution)/shard_map/combine_rows/pallas_call | solution.py:236
  584.0 1.9 pad_add_fusion.2.meta
  585.8 58.4 %gather_rows.6 = (bf16[32768,1536]{1,0:T(8,128)(2,1)}, bf16[32768,1536]{1,0:T(8,128)(2,1)}, f32[4096,8,128]{2,1,0:T(8,128)}) custom-call(s32[96]{0:T(128)} %get-tuple-element.238.blk_e, s32[96]{0:T(128)} %get-tuple-element.223.blk_k, s32[2]{0:T(128)} %pad_add_fusion.2.meta, ...), custom_call_target="tpu_custom_call", output_to_operand_aliasing={{0}: (6, {}), {1}: (7, {}), {2}: (8, {})} | custom-call | flops 60000002048 | bytes 120000000 | tf_op jit(solution)/shard_map/gather_rows/pallas_call | solution.py:89
  644.2 53.8 %experts.6 = (bf16[24576,1536]{1,0:T(8,128)(2,1)}, bf16[24576,1536]{1,0:T(8,128)(2,1)}, f32[24576,128]{1,0:T(8,128)}, bf16[32768,512]{1,0:T(8,128)(2,1)}, bf16[3...) custom-call(s32[96]{0:T(128)} %get-tuple-element.238.blk_e, ...), custom_call_target="tpu_custom_call", output_to_operand_aliasing={{3}: (8, {}), {4}: (9, {}), {5}: (10, {})} | custom-call | flops 60000002048 | bytes 80000000 | tf_op jit(solution)/shard_map/experts/pallas_call | solution.py:154
  698.1 66.1 %combine_rows.6 = (f32[512,192,128]{2,1,0:T(8,128)}, f32[512,8,128]{2,1,0:T(8,128)}) custom-call(s32[96]{0:T(128)} %get-tuple-element.238.blk_e, s32[96]{0:T(128)} %get-tuple-element.223.blk_k, s32[2]{0:T(128)} %pad_add_fusion.2.meta, s32[24576]{0:T(1024)} %bitcast.217, bf16[24576,1536]{1,0:T(8,128)(2,1)} %get-tuple-element.91.o_hbm, ...), custom_call_target="tpu_custom_call" | custom-call | flops 80000000000 | bytes 120000000 | tf_op jit(solution)/shard_map/combine_rows/pallas_call | solution.py:236
  766.4 1.9 pad_add_fusion.3.meta
  768.3 58.4 %gather_rows.7 = (bf16[32768,1536]{1,0:T(8,128)(2,1)}, bf16[32768,1536]{1,0:T(8,128)(2,1)}, f32[4096,8,128]{2,1,0:T(8,128)}) custom-call(s32[96]{0:T(128)} %get-tuple-element.239.blk_e, s32[96]{0:T(128)} %get-tuple-element.222.blk_k, s32[2]{0:T(128)} %pad_add_fusion.3.meta, ...), custom_call_target="tpu_custom_call", output_to_operand_aliasing={{0}: (6, {}), {1}: (7, {}), {2}: (8, {})} | custom-call | flops 60000002048 | bytes 120000000 | tf_op jit(solution)/shard_map/gather_rows/pallas_call | solution.py:89
  826.7 53.8 %experts.7 = (bf16[24576,1536]{1,0:T(8,128)(2,1)}, bf16[24576,1536]{1,0:T(8,128)(2,1)}, f32[24576,128]{1,0:T(8,128)}, bf16[32768,512]{1,0:T(8,128)(2,1)}, bf16[3...) custom-call(s32[96]{0:T(128)} %get-tuple-element.239.blk_e, ...), custom_call_target="tpu_custom_call", output_to_operand_aliasing={{3}: (8, {}), {4}: (9, {}), {5}: (10, {})} | custom-call | flops 60000002048 | bytes 80000000 | tf_op jit(solution)/shard_map/experts/pallas_call | solution.py:154
  880.5 66.3 %combine_rows.7 = (f32[512,192,128]{2,1,0:T(8,128)}, f32[512,8,128]{2,1,0:T(8,128)}) custom-call(s32[96]{0:T(128)} %get-tuple-element.239.blk_e, s32[96]{0:T(128)} %get-tuple-element.222.blk_k, s32[2]{0:T(128)} %pad_add_fusion.3.meta, s32[24576]{0:T(1024)} %bitcast.213, bf16[24576,1536]{1,0:T(8,128)(2,1)} %get-tuple-element.103.o_hbm, ...), custom_call_target="tpu_custom_call" | custom-call | flops 80000000000 | bytes 120000000 | tf_op jit(solution)/shard_map/combine_rows/pallas_call | solution.py:236
  950.0 12.3 fusion.31
  962.3 6.6 copy.126
  968.8 6.6 copy.127
  975.4 3.1 slice_bitcast_fusion.11
  978.5 2.2 copy.135
  980.6 3.1 slice_bitcast_fusion.10
  983.7 2.2 copy.136
  985.8 3.1 slice_bitcast_fusion.9
  988.9 2.2 copy.137
  991.1 3.1 slice_bitcast_fusion.8
  994.2 2.8 copy.138
  997.0 2.2 pad_maximum_fusion.4
  999.2 44.2 %all-to-all-start = ((f32[8,4,512,8]{2,1,3,0:T(4,128)}), f32[8,4,512,8]{2,1,3,0:T(4,128)}, u32[]{:S(2)}, u32[]{:S(2)}) async-start(f32[8,4,512,8]{2,1,3,0:T(4,128)} %pad_maximum_fusion.4), calls=%async_computation.4 | async-start | bytes 1048576 | tf_op jit(solution)/shard_map/all_to_all | solution.py:411
  1043.4 121.1 %weight_grads.1 = (bf16[8,1536,512]{2,1,0:T(8,128)(2,1)}, bf16[8,1536,512]{2,1,0:T(8,128)(2,1)}, bf16[8,512,1536]{2,1,0:T(8,128)(2,1)}) custom-call(s32[128]{0:T(128)} %add_clamp_fusion.order, s32[128]{0:T(128)} %get-tuple-element.229.owner, s32[1]{0:T(128)} %bitcast.66.total, bf16[32768,1536]{1,0:T(8,128)(2,1)} %get-tuple-element.112.x, ...), custom_call_target="tpu_custom_call" | custom-call | flops 99999997952 | bytes 160000000 | tf_op jit(solution)/shard_map/weight_grads/pallas_call | solution.py:288
  1166.9 5.9 slice_bitcast_fusion.3
  1172.8 125.9 %reduce-scatter.7.cloned.1.call-done = f32[64,192,128]{2,1,0:T(8,128)} async-done(((f32[512,192,128]{2,1,0:T(8,128)}), f32[64,192,128]{2,1,0:T(8,128)}) %reduce-scatter.7.cloned.1.call-update) | async-done | bytes 6291472 | tf_op jit(solution)/shard_map/reduce_scatter | solution.py:402
  1298.7 6.0 slice_bitcast_fusion.2
  1304.6 272.1 %reduce-scatter.9.cloned.1.call-done = f32[64,192,128]{2,1,0:T(8,128)} async-done(((f32[512,192,128]{2,1,0:T(8,128)}), f32[64,192,128]{2,1,0:T(8,128)}) %reduce-scatter.9.cloned.1.call-update) | async-done | bytes 6291472 | tf_op jit(solution)/shard_map/reduce_scatter | solution.py:402
  1576.8 5.9 slice_bitcast_fusion.1
  1582.7 272.2 %reduce-scatter.11.cloned.1.call-done = f32[64,192,128]{2,1,0:T(8,128)} async-done(((f32[512,192,128]{2,1,0:T(8,128)}), f32[64,192,128]{2,1,0:T(8,128)}) %reduce-scatter.11.cloned.1.call-update) | async-done | bytes 6291472 | tf_op jit(solution)/shard_map/reduce_scatter | solution.py:402
  1854.9 6.0 slice_bitcast_fusion
  1860.9 12.5 fusion.4
  1873.4 16.5 fusion.5
  1889.9 5.9 copy.173
  (125 shorter events, 25.1 us)
Async XLA Ops:
  7.2 44.9 %copy-start = (bf16[1024,1536]{1,0:T(8,128)(2,1)S(1)}, bf16[1024,1536]{1,0:T(8,128)(2,1)}, u32[]{:S(2)}) copy-start(bf16[1024,1536]{1,0:T(8,128)(2,1)} %param.18) | copy-start | bytes 9437188
  7.2 187.1 %all-gather.9.cloned.1.call-start = ((), (), s32[]{:S(2)}) async-start(), calls=%async_computation.5 | async-start | bytes 28311552 | tf_op jit(solution)/shard_map/all_gather | solution.py:374
  17.9 367.7 %all-gather.11.cloned.1.call-start = ((), (), s32[]{:S(2)}) async-start(), calls=%async_computation.7 | async-start | bytes 28311552 | tf_op jit(solution)/shard_map/all_gather | solution.py:374
  21.7 564.1 %all-gather.13.cloned.1.call-start = ((), (), s32[]{:S(2)}) async-start(), calls=%async_computation.9 | async-start | bytes 28311552 | tf_op jit(solution)/shard_map/all_gather | solution.py:374
  25.5 742.8 %all-gather.15.cloned.1.call-start = ((), (), s32[]{:S(2)}) async-start(), calls=%async_computation.11 | async-start | bytes 28311552 | tf_op jit(solution)/shard_map/all_gather | solution.py:374
  29.4 932.9 %all-reduce.7.cloned.1.call-start = ((), (), s32[]{:S(2)}) async-start(), calls=%async_computation.13 | async-start | bytes 37748736 | tf_op jit(solution)/shard_map/psum | solution.py:415
  29.4 11.9 copy-start.17
  70.6 12.2 copy-start.19
  70.6 23.0 %slice-start = ((s8[6291456]{0:T(1024)(128)(4,1)}), s8[4194304]{0:T(1024)(128)(4,1)S(1)}, s32[]{:S(2)}) async-start(s8[6291456]{0:T(1024)(128)(4,1)} %bitcast.198), calls=%async_computation.14 | async-start | bytes 8388608
  82.8 10.8 slice-start.1
  82.8 10.8 copy-start.18
  102.4 0.8 copy-start.9
  102.4 1064.4 %reduce-scatter.5.cloned.1.call-start = ((), (), s32[]{:S(2)}) async-start(), calls=%async_computation.6 | async-start | bytes 56623104 | tf_op jit(solution)/shard_map/reduce_scatter | solution.py:402
  103.1 26.0 %copy-start.16 = (s32[8]{0:T(128)}, s32[8]{0:T(128)S(1)}, u32[]{:S(2)}) copy-start(s32[8]{0:T(128)S(1)} %iota_add_fusion) | copy-start | bytes 100
  123.9 0.8 copy-start.1
  133.0 56.3 %copy-start.13 = (s32[4,8]{1,0:T(4,128)}, s32[4,8]{1,0:T(4,128)S(1)}, u32[]{:S(2)}) copy-start(s32[4,8]{1,0:T(4,128)S(1)} %get-tuple-element.212) | copy-start | bytes 388
  133.2 37.8 %copy-start.11 = (s32[4,8]{1,0:T(4,128)}, s32[4,8]{1,0:T(4,128)S(1)}, u32[]{:S(2)}) copy-start(s32[4,8]{1,0:T(4,128)S(1)} %reduce_window_sum.27) | copy-start | bytes 388
  156.7 14.3 copy-start.2
  381.6 0.9 copy-start.5
  381.6 1.6 copy-start.8
  381.6 917.1 %reduce-scatter.7.cloned.1.call-start = ((), (), s32[]{:S(2)}) async-start(), calls=%async_computation.8 | async-start | bytes 56623104 | tf_op jit(solution)/shard_map/reduce_scatter | solution.py:402
  581.7 0.9 copy-start.4
  581.7 1.6 copy-start.7
  581.7 995.0 %reduce-scatter.9.cloned.1.call-start = ((), (), s32[]{:S(2)}) async-start(), calls=%async_computation.10 | async-start | bytes 56623104 | tf_op jit(solution)/shard_map/reduce_scatter | solution.py:402
  764.1 0.9 copy-start.3
  764.1 1.6 copy-start.6
  764.2 1090.7 %reduce-scatter.11.cloned.1.call-start = ((), (), s32[]{:S(2)}) async-start(), calls=%async_computation.12 | async-start | bytes 56623104 | tf_op jit(solution)/shard_map/reduce_scatter | solution.py:402
  946.8 0.6 copy-start.12
  946.8 0.7 copy-start.14
  946.8 0.7 copy-start.15
  999.2 165.4 %all-to-all-start = ((f32[8,4,512,8]{2,1,3,0:T(4,128)}), f32[8,4,512,8]{2,1,3,0:T(4,128)}, u32[]{:S(2)}, u32[]{:S(2)}) async-start(f32[8,4,512,8]{2,1,3,0:T(4,128)} %pad_maximum_fusion.4), calls=%async_computation.4 | async-start | bytes 1048576 | tf_op jit(solution)/shard_map/all_to_all | solution.py:411
  1043.4 122.3 %copy-start.10 = (s32[2048,6]{0,1:T(8,128)S(1)}, s32[2048,6]{0,1:T(8,128)}, u32[]{:S(2)}) copy-start(s32[2048,6]{0,1:T(8,128)} %param.11) | copy-start | bytes 147460
Sparse Core Ops, SparseCore 0:
  18.0 126.1 all-gather.8
  146.0 119.6 all-gather.10
  268.1 119.6 all-gather.12
  390.0 119.6 all-gather.14
  514.9 227.5 all-reduce.6
  745.9 274.6 reduce-scatter.4
  1024.1 274.5 reduce-scatter.6
  1302.2 274.5 reduce-scatter.8
  1580.3 274.5 reduce-scatter.10
